TPU v7x, 8 devices: a whole 2x2x1 slice. The times are simulated.
8 devices in a mesh: rep: 2 (over z, y), blk: 4 (over x, core).
Axes of the slice: x: 2, y: 2, z: 1, core: 2. Of those that a mesh axis runs over, the one named last changes fastest.
Arguments:
- ratings: float32 [512, 4096], P(None, ('rep', 'blk')), parts along dimension 1
- observed: int32 [512, 4096], P(None, ('rep', 'blk')), parts along dimension 1
- user_init: float32 [1024, 50], P(('rep', 'blk')), parts along dimension 0
- item_init: float32 [4096, 50], P(('rep', 'blk')), parts along dimension 0
- lr_scale: float32 [64, 4], replicated
Outputs:
- output 1: float32 [1024, 50], P(('rep', 'blk')), parts along dimension 0
- output 2: float32 [4096, 50], P(('rep', 'blk')), parts along dimension 0
There are 2 independent parts. A program takes and returns all parts, laid end to end along the dimension named above; an argument that names none is the same for every part.
All inputs are finite; a program needn't handle non-finite values.
Results may differ from a plain program's by a relative error of at most 0.001.
Values are sent between devices in bfloat16 or wider.
A program may use at most 1 GiB of HBM per device.

v0:
```python
import math
import jax
import jax.numpy as jnp
from jax import lax
from jax.sharding import PartitionSpec as P

LAMBDA = 0.05


def stratum_steps(users_cur, items_cur, rate_blk, mask_blk, lr_row, base_eta):
    def one_step(step_idx, step_state):
        users_now, items_now = step_state
        users_bf = users_now.astype(jnp.bfloat16)
        items_bf = items_now.astype(jnp.bfloat16)
        approx = jnp.einsum("ar,br->ab", users_bf, items_bf, preferred_element_type=jnp.float32)
        errors = jnp.where(mask_blk != 0, approx - rate_blk, 0.0).astype(jnp.bfloat16)
        grad_u = jnp.einsum("ab,br->ar", errors, items_bf, preferred_element_type=jnp.float32) + LAMBDA * users_now
        grad_v = jnp.einsum("ab,ar->br", errors, users_bf, preferred_element_type=jnp.float32) + LAMBDA * items_now
        step_size = base_eta * lr_row[step_idx]
        return users_now - step_size * grad_u, items_now - step_size * grad_v

    return lax.fori_loop(0, lr_row.shape[0], one_step, (users_cur, items_cur))


def solution(mesh):
    group_size = mesh.shape["blk"]
    send_perm = [(source, (source - 1) % group_size) for source in range(group_size)]

    def local_run(rate_loc, mask_loc, user_loc, item_loc, lr_scale):
        block_rows, rank_dim = user_loc.shape
        cols_dev = item_loc.shape[0]
        base_eta = math.sqrt(rank_dim) / (4.0 * (cols_dev + 2 * rank_dim))
        my_index = lax.axis_index("blk")

        def sub_epoch(t_index, loop_state):
            users_cur, items_cur = loop_state
            row_start = ((my_index + t_index) % group_size) * block_rows
            rate_blk = lax.dynamic_slice_in_dim(rate_loc, row_start, block_rows, 0)
            mask_blk = lax.dynamic_slice_in_dim(mask_loc, row_start, block_rows, 0)
            users_cur, items_cur = stratum_steps(users_cur, items_cur, rate_blk, mask_blk, lr_scale[t_index], base_eta)
            users_cur = lax.ppermute(users_cur, "blk", send_perm)
            return users_cur, items_cur

        return lax.fori_loop(0, lr_scale.shape[0], sub_epoch, (user_loc, item_loc))

    spec_cols = P(None, ("rep", "blk"))
    spec_rows = P(("rep", "blk"), None)
    mapped = jax.shard_map(local_run, mesh=mesh, in_specs=(spec_cols, spec_cols, spec_rows, spec_rows, P(None, None)), out_specs=(spec_rows, spec_rows), check_vma=False)
    return mapped
```

profile of v0, /device:TPU:1, one launch (start us, length us, event | category | flops | bytes accessed | tf_op | source)
XLA Modules:
  0.0 787.9 jit_solution(982333566068158979)
XLA Ops:
  1.5 785.7 %while.56 = (s32[]{:T(128)}, f32[128,50]{0,1:T(8,128)S(1)}, f32[512,50]{0,1:T(8,128)S(1)}, s32[]{:T(128)}, s32[512,512]{1,0:T(8,128)}, /*index=5*/f32[512,512]{1...) while((s32[]{:T(128)}, f32[128,50]{0,1:T(8,128)S(1)}, ...), condition=%wide.region_3.4_spmd, body=%wide.region_0.3_spmd.sunk | while | flops 20114964 | bytes 2683469 | solution.py:44
  16.6 7.0 while.57
  28.9 7.0 while.57
  41.2 7.0 while.57
  65.7 7.0 while.57
  78.0 7.0 while.57
  90.2 7.0 while.57
  114.7 7.0 while.57
  127.0 7.0 while.57
  139.3 7.0 while.57
  163.8 7.0 while.57
  176.1 7.0 while.57
  188.3 7.0 while.57
  212.8 7.0 while.57
  225.1 7.0 while.57
  237.4 7.0 while.57
  261.9 7.0 while.57
  274.2 7.0 while.57
  286.4 7.0 while.57
  311.0 7.0 while.57
  323.2 7.0 while.57
  335.5 7.0 while.57
  360.0 7.0 while.57
  372.3 7.0 while.57
  384.5 7.0 while.57
  409.1 7.0 while.57
  421.3 7.0 while.57
  433.6 7.0 while.57
  458.1 7.0 while.57
  470.4 7.0 while.57
  482.6 7.0 while.57
  507.2 7.0 while.57
  519.4 7.0 while.57
  531.7 7.0 while.57
  556.2 7.0 while.57
  568.5 7.0 while.57
  580.7 7.0 while.57
  605.3 7.0 while.57
  617.5 7.0 while.57
  629.8 7.0 while.57
  654.3 7.0 while.57
  666.6 7.0 while.57
  678.8 7.0 while.57
  703.4 7.0 while.57
  715.6 7.0 while.57
  727.9 7.0 while.57
  752.4 7.0 while.57
  777.0 7.0 while.57
  (1692 shorter events, 747.2 us)
Async XLA Ops:
  10.5 4.2 collective-permute-start
  23.6 3.3 collective-permute-start
  35.9 3.3 collective-permute-start
  48.1 3.3 collective-permute-start
  60.4 3.3 collective-permute-start
  72.7 3.3 collective-permute-start
  84.9 3.3 collective-permute-start
  97.2 3.3 collective-permute-start
  109.5 3.3 collective-permute-start
  121.7 3.3 collective-permute-start
  158.5 3.3 collective-permute-start
  183.0 3.3 collective-permute-start
  195.3 3.3 collective-permute-start
  219.8 3.3 collective-permute-start
  244.3 3.3 collective-permute-start
  256.6 3.3 collective-permute-start
  281.1 3.3 collective-permute-start
  293.4 3.3 collective-permute-start
  317.9 3.3 collective-permute-start
  330.2 3.3 collective-permute-start
  342.5 3.3 collective-permute-start
  354.7 3.3 collective-permute-start
  367.0 3.3 collective-permute-start
  379.2 3.3 collective-permute-start
  403.8 3.3 collective-permute-start
  416.0 3.3 collective-permute-start
  428.3 3.3 collective-permute-start
  440.6 3.3 collective-permute-start
  452.8 3.3 collective-permute-start
  465.1 3.3 collective-permute-start
  501.9 3.3 collective-permute-start
  526.4 3.3 collective-permute-start
  538.7 3.3 collective-permute-start
  563.2 3.3 collective-permute-start
  587.7 3.3 collective-permute-start
  600.0 3.3 collective-permute-start
  624.5 3.3 collective-permute-start
  636.8 3.3 collective-permute-start
  661.3 3.3 collective-permute-start
  673.6 3.3 collective-permute-start
  685.8 3.3 collective-permute-start
  698.1 3.3 collective-permute-start
  710.3 3.3 collective-permute-start
  722.6 3.3 collective-permute-start
  747.1 3.3 collective-permute-start
  759.4 3.3 collective-permute-start
  771.7 3.3 collective-permute-start
  783.9 3.3 collective-permute-start
  (21 other events, 56.9 us)
where the time goes:
time: 794 us; the launch traced here: 788 us
  local copies, waits for them, and re-layouts  276 us (35%)
  waiting for transfers between devices  211 us (27%)
  loops' own time  158 us (20%)
  matrix products  140 us (18%)
    ppermute x64, waiting for transfers between devices, sub_epoch(): users_cur = lax.ppermute(users_cur, 'blk', send_perm)  211 us
    another operation x64, loops' own time, stratum_steps(): return lax.fori_loop(0, lr_row.shape[0], one_step, (users_cur, items_cur))  156 us
    dynamic_slice x256, local copies, waits for them, and re-layouts, one_step(): step_size = base_eta * lr_row[step_idx]  148 us
    dynamic_slice x64, local copies, waits for them, and re-layouts, sub_epoch(): mask_blk = lax.dynamic_slice_in_dim(mask_loc, row_start, block_rows, 0)  62.4 us
    dynamic_slice x64, local copies, waits for them, and re-layouts, sub_epoch(): rate_blk = lax.dynamic_slice_in_dim(rate_loc, row_start, block_rows, 0)  62.3 us
    dot_general x256, matrix products, one_step(): jnp.einsum('ar,br->ab', users_bf, items_bf, preferred_element_type=jnp.fl...  54.2 us
    dot_general x256, matrix products, one_step(): jnp.einsum('ab,ar->br', errors, users_bf, preferred_element_type=jnp.floa...  43.4 us
    dot_general x256, matrix products, one_step(): jnp.einsum('ab,br->ar', errors, items_bf, preferred_element_type=jnp.floa...  42.3 us
  transfers between devices with their start and end apart: 64, of which 64 were waited for; matrix products, arithmetic and copies ran while one was open for 0% of the time, Pallas kernels for 0%

commit v1 on v0

v1 whole, which is shorter than its diff:
```python
import functools
import math

import jax
import jax.numpy as jnp
from jax import lax
from jax.experimental import pallas as pl
from jax.experimental.pallas import tpu as pltpu
from jax.sharding import PartitionSpec as P

LAMBDA = 0.05
LEADER = 1
STEPS = 4
KPAD = 64
F32 = jnp.float32
BF16 = jnp.bfloat16
MESH_ID = pl.DeviceIdType.MESH


def make_order(nb, subs, len_a=64, len_b=96, a_to_b=226, b_to_c=211, len_c=56):
    def deps(s, i):
        if s == 0:
            return []
        return [(s - 1, i)] + ([(s - 1, (i - 1) % nb)] if s % STEPS == 0 else [])

    todo_a = {(s, i) for s in range(STEPS * subs) for i in range(nb)}
    todo_b, start_a, done_c, events, now = set(), {}, {}, [], 0
    while todo_a or todo_b:
        cand = []
        first = min((s for s, _ in todo_a), default=0)
        for s, i in todo_a:
            if s <= first + 1 and all(d in done_c for d in deps(s, i)):
                ready = max([done_c[d] for d in deps(s, i)], default=0)
                cand.append((max(ready, now), s * 10 + 5, nb - i, "A", s, i))
        for s, i in todo_b:
            cand.append((max(start_a[s, i] + a_to_b, now), s * 10, nb - i, "B", s, i))
        begin, _, _, kind, s, i = min(cand)
        if kind == "A":
            start_a[s, i] = begin
            todo_a.remove((s, i))
            todo_b.add((s, i))
            now = begin + len_a
            events.append((begin, 0, kind, s, i))
        else:
            todo_b.remove((s, i))
            now = begin + len_b
            done_c[s, i] = now + b_to_c + len_c
            events.append((begin, 1, kind, s, i))
            events.append((now + b_to_c, 2, "C", s, i))
    return [e[2:] for e in sorted(events)]


def dot(a, b):
    return jnp.dot(a, b, preferred_element_type=F32)


def dot_nt(a, b):
    return lax.dot_general(a, b, (((1,), (1,)), ((), ())), preferred_element_type=F32)


def kernel(nb, rank, base_eta, lr, rate, ut_in, vt_in, ut_out, vt_out,
           r_all, m_all, ut_land, vt_land, u32, v32, ub, utb, vb,
           r_sem, s_sem, u_sem, v_sem, us_sem, vs_sem, ou_sem, ov_sem, ous_sem, ovs_sem):
    me = lax.axis_index("blk")
    rows = r_all.shape[2]
    subs = lr.shape[0]
    barrier = pltpu.get_barrier_semaphore()

    def block_copy(w):
        start = pl.multiple_of(lax.rem(me + w, nb) * rows, rows)
        return rate.at[pl.ds(start, rows)]

    @pl.when(me != LEADER)
    def _():
        pl.semaphore_signal(barrier, inc=1, device_id={"blk": LEADER}, device_id_type=MESH_ID)
        pl.semaphore_wait(barrier, 1)
        to = dict(device_id={"blk": LEADER}, device_id_type=MESH_ID)
        cps = [
            pltpu.make_async_remote_copy(ut_in, ut_land.at[me], us_sem, u_sem.at[me], **to),
            pltpu.make_async_remote_copy(vt_in, vt_land.at[me], vs_sem, v_sem.at[me], **to),
        ]
        for w in range(nb):
            cps.append(pltpu.make_async_remote_copy(block_copy(w), r_all.at[w, me], s_sem.at[w], r_sem.at[w, me], **to))
        for cp in cps:
            cp.start()
        for cp in cps:
            cp.wait_send()
        pltpu.make_async_copy(ut_out, ut_out, ou_sem).wait()
        pltpu.make_async_copy(vt_out, vt_out, ov_sem).wait()

    @pl.when(me == LEADER)
    def _():
        others = [j for j in range(nb) if j != LEADER]
        for j in others:
            pl.semaphore_signal(barrier, inc=1, device_id={"blk": j}, device_id_type=MESH_ID)
        pl.semaphore_wait(barrier, nb - 1)
        pltpu.make_async_copy(ut_in, ut_land.at[LEADER], u_sem.at[LEADER]).start()
        pltpu.make_async_copy(vt_in, vt_land.at[LEADER], v_sem.at[LEADER]).start()
        for w in range(nb):
            pltpu.make_async_copy(block_copy(w), r_all.at[w, LEADER], r_sem.at[w, LEADER]).start()

        for i in range(nb):
            pltpu.make_async_copy(ut_land.at[i], ut_land.at[i], u_sem.at[i]).wait()
            pltpu.make_async_copy(vt_land.at[i], vt_land.at[i], v_sem.at[i]).wait()
            v32[i] = jnp.zeros(v32.shape[1:], F32)
            v32[i, :rank] = vt_land[i]
            vb[i] = v32[i].astype(BF16)
            ut = jnp.concatenate([ut_land[i], jnp.zeros((rows - rank, rows), F32)], axis=0)
            u32[i] = ut.T[:, :KPAD]
            ub[i] = ut.T[:, :KPAD].astype(BF16)
            utb[i] = ut[:KPAD].astype(BF16)

        def run(order, t0, w_of, j_of):
            prod, gu, gv = {}, {}, {}
            for kind, s, i in order:
                sub = s // STEPS
                j, w = j_of(sub, i), w_of(sub)
                if kind == "A":
                    prod[s, i] = dot(ub[i], vb[j])
                elif kind == "B":
                    err = (prod.pop((s, i)) - r_all[w, j]).astype(BF16) * m_all[w, j]
                    gu[s, i] = dot_nt(err, vb[j])
                    gv[s, i] = dot(utb[i], err)
                else:
                    eta = lr[t0 + sub, s % STEPS] * base_eta
                    keep = 1.0 - eta * LAMBDA
                    u_new = u32[i] * keep - eta * gu.pop((s, i))
                    u32[i] = u_new
                    u_bf = u_new.astype(BF16)
                    ub[i] = u_bf
                    utb[i] = u_bf.T
                    v_new = v32[j] * keep - eta * gv.pop((s, i))
                    v32[j] = v_new
                    vb[j] = v_new.astype(BF16)

        order_1 = make_order(nb, 1)
        order_n = make_order(nb, nb)

        def first_epoch(w, carry):
            for j in range(nb):
                pltpu.make_async_copy(r_all.at[w, j], r_all.at[w, j], r_sem.at[w, j]).wait()
                coded = r_all[w, j]
                seen = coded < jnp.inf
                m_all[w, j] = jnp.where(seen, 1.0, 0.0).astype(BF16)
                r_all[w, j] = jnp.where(seen, coded, 0.0)
            run(order_1, w, lambda sub: w, lambda sub, i: lax.rem(i - w + nb, nb))
            return carry

        def epoch(e, carry):
            run(order_n, e * nb, lambda sub: sub, lambda sub, i: (i - sub) % nb)
            return carry

        lax.fori_loop(0, nb, first_epoch, 0)
        lax.fori_loop(1, subs // nb, epoch, 0)

        for i in range(nb):
            ut = jnp.concatenate([u32[i], jnp.zeros((rows, rows - KPAD), F32)], axis=1).T
            ut_land[i] = ut[:rank]
            vt_land[i] = v32[i, :rank]
        cps = []
        for n, j in enumerate(others):
            to = dict(device_id={"blk": j}, device_id_type=MESH_ID)
            cps.append(pltpu.make_async_remote_copy(vt_land.at[j], vt_out, ovs_sem.at[n], ov_sem, **to))
            cps.append(pltpu.make_async_remote_copy(ut_land.at[j], ut_out, ous_sem.at[n], ou_sem, **to))
        for cp in cps:
            cp.start()
        ut_out[...] = ut_land[LEADER]
        vt_out[...] = vt_land[LEADER]
        for cp in cps:
            cp.wait_send()


def solution(mesh):
    nb = mesh.shape["blk"]

    def local_run(rate_loc, mask_loc, user_loc, item_loc, lr_scale):
        rows, rank = user_loc.shape
        cols = item_loc.shape[0]
        base_eta = math.sqrt(rank) / (4.0 * (cols + 2 * rank))
        coded = jnp.where(mask_loc != 0, rate_loc, jnp.inf)
        vmem = pl.BlockSpec(memory_space=pltpu.VMEM)
        dma = pltpu.SemaphoreType.DMA
        ut, vt = pl.pallas_call(
            functools.partial(kernel, nb, rank, base_eta),
            out_shape=(jax.ShapeDtypeStruct((rank, rows), F32), jax.ShapeDtypeStruct((rank, cols), F32)),
            in_specs=[pl.BlockSpec(memory_space=pltpu.SMEM), pl.BlockSpec(memory_space=pl.ANY), vmem, vmem],
            out_specs=(vmem, vmem),
            scratch_shapes=[
                pltpu.VMEM((nb, nb, rows, cols), F32),
                pltpu.VMEM((nb, nb, rows, cols), BF16),
                pltpu.VMEM((nb, rank, rows), F32),
                pltpu.VMEM((nb, rank, cols), F32),
                pltpu.VMEM((nb, rows, KPAD), F32),
                pltpu.VMEM((nb, KPAD, cols), F32),
                pltpu.VMEM((nb, rows, KPAD), BF16),
                pltpu.VMEM((nb, KPAD, rows), BF16),
                pltpu.VMEM((nb, KPAD, cols), BF16),
                dma((nb, nb)), dma((nb,)), dma((nb,)), dma((nb,)), dma, dma,
                dma, dma, dma((nb - 1,)), dma((nb - 1,)),
            ],
            compiler_params=pltpu.CompilerParams(collective_id=0, has_side_effects=True),
            name="dsgd",
        )(lr_scale, coded, user_loc.T, item_loc.T)
        return ut.T, vt.T

    spec_cols = P(None, ("rep", "blk"))
    spec_rows = P(("rep", "blk"), None)
    return jax.shard_map(
        local_run,
        mesh=mesh,
        in_specs=(spec_cols, spec_cols, spec_rows, spec_rows, P(None, None)),
        out_specs=(spec_rows, spec_rows),
        check_vma=False,
    )
```

time: 794 us -> 144 us (0.18)
  local copies, waits for them, and re-layouts: 276 us -> 4.29 us
  waiting for transfers between devices: 211 us -> 0 us
  loops' own time: 158 us -> 0 us
  matrix products: 140 us -> 0 us
  Pallas kernels: 0 us -> 136 us
    dynamic_slice x384 -> x0, local copies, waits for them, and re-layouts: 273 us -> none  [the longest x256 148 us: one_step(): step_size = base_eta * lr_row[step_idx]]
    ppermute x64 -> x0, waiting for transfers between devices: 211 us -> none  [sub_epoch(): users_cur = lax.ppermute(users_cur, 'blk', send_perm)]
    another operation x65 -> x0, loops' own time: 158 us -> none  [the longest x64 156 us: stratum_steps(): return lax.fori_loop(0, lr_row.shape[0], one_step, (users_cur, items_cur))]
    dot_general x768 -> x0, matrix products: 140 us -> none  [the longest x256 54.2 us: one_step(): jnp.einsum('ar,br->ab', users_bf, items_bf, preferred_element_type=jnp.fl...]
    pallas_call x0 -> x1, Pallas kernels: none -> 136 us  [local_run(): pl.pallas_call(functools.partial(kernel, nb, rank, base_eta), out_shape=(...]
  transfers between devices with their start and end apart: 64 -> 0, of which waited for: 64 -> 0; matrix products, arithmetic and copies ran while one was open for 0% -> 0% of each run, Pallas kernels for 0% -> 0%
where the time goes in v1:
time: 144 us
  Pallas kernels  136 us (94%)
  local copies, waits for them, and re-layouts  4.29 us (3%)
  other arithmetic  2.72 us (2%)
    pallas_call x1, Pallas kernels, local_run(): pl.pallas_call(functools.partial(kernel, nb, rank, base_eta), out_shape=(...  136 us
    unnamed x5, local copies, waits for them, and re-layouts  4.29 us

profile of v1, /device:TPU:1, one launch (start us, length us, event | category | flops | bytes accessed | tf_op | source)
XLA Modules:
  0.0 144.0 jit_solution(3722272153390700506)
XLA Ops:
  0.6 0.0 copy-start
  0.6 0.7 copy-done
  1.3 0.7 copy.7.lr
  2.0 2.7 %compare_select_fusion.rate = f32[512,512]{1,0:T(8,128)} fusion(f32[512,512]{1,0:T(8,128)} %param.5, s32[512,512]{1,0:T(8,128)} %param.6), kind=kLoop, calls=%fused_computation | loop fusion | flops 524288 | bytes 3145728 | tf_op jit(solution)/shard_map/jit(_where)/select_n | solution.py:180
  4.7 136.3 %dsgd.1 = (f32[50,128]{1,0:T(8,128)}, f32[50,512]{1,0:T(8,128)}) custom-call(f32[64,4]{1,0:T(8,128)} %copy.7.lr, f32[512,512]{1,0:T(8,128)} %compare_select_fusion.rate, f32[50,128]{1,0:T(8,128)} %bitcast.7, f32[50,512]{1,0:T(8,128)} %bitcast.4), custom_call_target="tpu_custom_call" | custom-call | tf_op jit(solution)/shard_map/dsgd/pallas_call | solution.py:183
  141.1 1.4 copy.10
  142.5 1.6 %copy.11 = f32[512,50]{0,1:T(8,128)} copy(f32[512,50]{0,1:T(8,128)} %bitcast.5) | data formatting | bytes 204800
Async XLA Ops:
  0.6 0.7 copy-start

commit v2 on v1

v2 whole, which is shorter than its diff:
```python
import functools
import math
import random

import jax
import jax.numpy as jnp
from jax import lax
from jax.experimental import pallas as pl
from jax.experimental.pallas import tpu as pltpu
from jax.sharding import PartitionSpec as P

LAMBDA = 0.05
LEADER = 1
STEPS = 4
KPAD = 64
UNROLL = 12
LEN_A, LEN_B, A_TO_B, B_TO_C, LEN_C = 64, 96, 226, 211, 80
F32 = jnp.float32
BF16 = jnp.bfloat16
MESH_ID = pl.DeviceIdType.MESH


def play(order, nb):
    now, start, done = 0, {}, {}
    for kind, s, i in order:
        if kind == "A":
            ready = 0
            if s > 0:
                before = [(s - 1, i)] + ([(s - 1, (i - 1) % nb)] if s % STEPS == 0 else [])
                if any(d not in done for d in before):
                    return None
                ready = max(done[d] for d in before)
            start[kind, s, i] = max(now, ready)
            now = start[kind, s, i] + LEN_A
        else:
            if ("A", s, i) not in start:
                return None
            start[kind, s, i] = max(now, start["A", s, i] + A_TO_B)
            now = start[kind, s, i] + LEN_B
            done[s, i] = now + B_TO_C + LEN_C
    return max(done.values()), start


def make_order(nb, subs, tries):
    users = [(s, i) for s in range(STEPS * subs) for i in reversed(range(nb))]
    best = []
    for n in range(len(users) + 1):
        best += [("A", *users[n])] if n < len(users) else []
        best += [("B", *users[n - 1])] if n > 0 else []
    rnd = random.Random(0)
    cur, length = best, play(best, nb)[0]
    low = length
    for it in range(tries):
        new = list(cur)
        at = rnd.randrange(len(new))
        item = new.pop(at)
        new.insert(max(0, at + rnd.choice((-4, -3, -2, -1, 1, 2, 3, 4))), item)
        played = play(new, nb)
        if played is None:
            continue
        temp = 60 * (1 - it / tries) + 0.5
        if played[0] <= length or rnd.random() < math.exp((length - played[0]) / temp):
            cur, length = new, played[0]
            if length < low:
                best, low = new, length
    start = play(best, nb)[1]
    events = [(t, 1, *key) for key, t in start.items()]
    events += [(t + LEN_B + B_TO_C, 0, "C", s, i) for (kind, s, i), t in start.items() if kind == "B"]
    return [e[2:] for e in sorted(events)]


def dot(a, b):
    return jnp.dot(a, b, preferred_element_type=F32)


def dot_nt(a, b):
    return lax.dot_general(a, b, (((1,), (1,)), ((), ())), preferred_element_type=F32)


def kernel(nb, rank, base_eta, lr, rate, mask, ut_in, vt_in, ut_out, vt_out,
           r_all, m_all, r_own, m_own, ut_land, vt_land, u32, v32, ub, utb, vb,
           rl_sem, ml_sem, r_sem, s_sem, u_sem, v_sem, us_sem, vs_sem, ou_sem, ov_sem, ous_sem, ovs_sem):
    me = lax.axis_index("blk")
    rows, cols = r_all.shape[2:]
    subs = lr.shape[1]
    half = cols // 2
    halves = [slice(h * half, (h + 1) * half) for h in range(2)]
    barrier = pltpu.get_barrier_semaphore()

    loads = []
    for w in range(nb):
        start = pl.multiple_of(lax.rem(me + w, nb) * rows, rows)
        loads.append((
            pltpu.make_async_copy(rate.at[pl.ds(start, rows)], r_own.at[w], rl_sem.at[w]),
            pltpu.make_async_copy(mask.at[pl.ds(start, rows)], m_own.at[w], ml_sem.at[w]),
        ))
    for pair in loads:
        for cp in pair:
            cp.start()

    @pl.when(me != LEADER)
    def _():
        to = dict(device_id={"blk": LEADER}, device_id_type=MESH_ID)
        pl.semaphore_signal(barrier, inc=1, **to)

        def encode(w):
            for cp in loads[w]:
                cp.wait()
            r_own[w] = jnp.where(m_own[w] != 0, r_own[w], jnp.inf)

        encode(0)
        encode(1)
        pl.semaphore_wait(barrier, 1)
        cps = [
            pltpu.make_async_remote_copy(ut_in, ut_land.at[me], us_sem, u_sem.at[me], **to),
            pltpu.make_async_remote_copy(vt_in, vt_land.at[me], vs_sem, v_sem.at[me], **to),
        ]
        for w in range(nb):
            cps.append(pltpu.make_async_remote_copy(r_own.at[w], r_all.at[w, me], s_sem.at[w], r_sem.at[w, me], **to))
        for cp in cps[:3]:
            cp.start()
        encode(2)
        cps[3].start()
        encode(3)
        for cp in cps[4:]:
            cp.start()
        for cp in cps:
            cp.wait_send()
        pltpu.make_async_copy(ut_out, ut_out, ou_sem).wait()
        pltpu.make_async_copy(vt_out, vt_out, ov_sem).wait()

    @pl.when(me == LEADER)
    def _():
        others = [j for j in range(nb) if j != LEADER]
        for j in others:
            pl.semaphore_signal(barrier, inc=1, device_id={"blk": j}, device_id_type=MESH_ID)
        ut_land[LEADER] = ut_in[...]
        vt_land[LEADER] = vt_in[...]
        for w in range(nb):
            for cp in loads[w]:
                cp.wait()
            m_all[w, LEADER] = m_own[w].astype(F32).astype(BF16)
            r_all[w, LEADER] = r_own[w]
        pl.semaphore_wait(barrier, nb - 1)

        for i in range(nb):
            if i != LEADER:
                pltpu.make_async_copy(ut_land.at[i], ut_land.at[i], u_sem.at[i]).wait()
                pltpu.make_async_copy(vt_land.at[i], vt_land.at[i], v_sem.at[i]).wait()
            v32[i] = jnp.zeros(v32.shape[1:], F32)
            v32[i, :rank] = vt_land[i]
            vb[i] = v32[i].astype(BF16)
            ut = jnp.concatenate([ut_land[i], jnp.zeros((rows - rank, rows), F32)], axis=0)
            u32[i] = ut.T[:, :KPAD]
            ub[i] = ut.T[:, :KPAD].astype(BF16)
            utb[i] = ut[:KPAD].astype(BF16)

        def run(order, t0, w_of, j_of):
            prod, grads = {}, {}
            for kind, s, i in order:
                sub = s // STEPS
                j, w = j_of(sub, i), w_of(sub)
                if kind == "A":
                    prod[s, i] = [dot(ub[i], vb[j, :, h]) for h in halves]
                elif kind == "B":
                    errs = [
                        (a - r_all[w, j, :, h]).astype(BF16) * m_all[w, j, :, h]
                        for a, h in zip(prod.pop((s, i)), halves)
                    ]
                    gu = [dot_nt(err, vb[j, :, h]) for err, h in zip(errs, halves)]
                    grads[s, i] = gu, [dot(utb[i], err) for err in errs]
                else:
                    eta = lr[s % STEPS, t0 + sub] * base_eta
                    keep = 1.0 - eta * LAMBDA
                    gu, gv = grads.pop((s, i))
                    u_new = u32[i] * keep - eta * gu[0] - eta * gu[1]
                    u32[i] = u_new
                    u_bf = u_new.astype(BF16)
                    ub[i] = u_bf
                    utb[i] = u_bf.T
                    for g, h in zip(gv, halves):
                        v_new = v32[j, :, h] * keep - eta * g
                        v32[j, :, h] = v_new
                        vb[j, :, h] = v_new.astype(BF16)

        order_1 = make_order(nb, 1, 3000)
        order_n = make_order(nb, UNROLL, 0)

        def first_epoch(w, carry):
            for j in [j for j in range(nb) if j != LEADER]:
                pltpu.make_async_copy(r_all.at[w, j], r_all.at[w, j], r_sem.at[w, j]).wait()
                coded = r_all[w, j]
                seen = coded < jnp.inf
                m_all[w, j] = jnp.where(seen, 1.0, 0.0).astype(BF16)
                r_all[w, j] = jnp.where(seen, coded, 0.0)
            run(order_1, w, lambda sub: w, lambda sub, i: lax.rem(i - w + nb, nb))
            return carry

        def later(n, carry):
            run(order_n, nb + n * UNROLL, lambda sub: sub % nb, lambda sub, i: (i - sub) % nb)
            return carry

        lax.fori_loop(0, nb, first_epoch, 0)
        lax.fori_loop(0, (subs - nb) // UNROLL, later, 0)

        for i in range(nb):
            ut = jnp.concatenate([u32[i], jnp.zeros((rows, rows - KPAD), F32)], axis=1).T
            ut_land[i] = ut[:rank]
            vt_land[i] = v32[i, :rank]
        cps = []
        for n, j in enumerate(others):
            to = dict(device_id={"blk": j}, device_id_type=MESH_ID)
            cps.append(pltpu.make_async_remote_copy(vt_land.at[j], vt_out, ovs_sem.at[n], ov_sem, **to))
            cps.append(pltpu.make_async_remote_copy(ut_land.at[j], ut_out, ous_sem.at[n], ou_sem, **to))
        cps.reverse()
        for cp in cps:
            cp.start()
        mine = [
            pltpu.make_async_copy(ut_land.at[LEADER], ut_out, ou_sem),
            pltpu.make_async_copy(vt_land.at[LEADER], vt_out, ov_sem),
        ]
        for cp in mine:
            cp.start()
        for cp in mine:
            cp.wait()
        for cp in cps:
            cp.wait_send()


def solution(mesh):
    nb = mesh.shape["blk"]

    def local_run(rate_loc, mask_loc, user_loc, item_loc, lr_scale):
        rows, rank = user_loc.shape
        cols = item_loc.shape[0]
        base_eta = math.sqrt(rank) / (4.0 * (cols + 2 * rank))
        vmem = pl.BlockSpec(memory_space=pltpu.VMEM)
        hbm = pl.BlockSpec(memory_space=pl.ANY)
        dma = pltpu.SemaphoreType.DMA
        ut, vt = pl.pallas_call(
            functools.partial(kernel, nb, rank, base_eta),
            out_shape=(jax.ShapeDtypeStruct((rank, rows), F32), jax.ShapeDtypeStruct((rank, cols), F32)),
            in_specs=[pl.BlockSpec(memory_space=pltpu.SMEM), hbm, hbm, vmem, vmem],
            out_specs=(hbm, hbm),
            scratch_shapes=[
                pltpu.VMEM((nb, nb, rows, cols), F32),
                pltpu.VMEM((nb, nb, rows, cols), BF16),
                pltpu.VMEM((nb, rows, cols), F32),
                pltpu.VMEM((nb, rows, cols), jnp.int32),
                pltpu.VMEM((nb, rank, rows), F32),
                pltpu.VMEM((nb, rank, cols), F32),
                pltpu.VMEM((nb, rows, KPAD), F32),
                pltpu.VMEM((nb, KPAD, cols), F32),
                pltpu.VMEM((nb, rows, KPAD), BF16),
                pltpu.VMEM((nb, KPAD, rows), BF16),
                pltpu.VMEM((nb, KPAD, cols), BF16),
                dma((nb,)), dma((nb,)),
                dma((nb, nb)), dma((nb,)), dma((nb,)), dma((nb,)), dma, dma,
                dma, dma, dma((nb - 1,)), dma((nb - 1,)),
            ],
            compiler_params=pltpu.CompilerParams(collective_id=0, has_side_effects=True),
            name="dsgd",
        )(lr_scale.T, rate_loc, mask_loc, user_loc.T, item_loc.T)
        return ut.T, vt.T

    spec_cols = P(None, ("rep", "blk"))
    spec_rows = P(("rep", "blk"), None)
    return jax.shard_map(
        local_run,
        mesh=mesh,
        in_specs=(spec_cols, spec_cols, spec_rows, spec_rows, P(None, None)),
        out_specs=(spec_rows, spec_rows),
        check_vma=False,
    )
```

time: 144 us -> 131 us (0.910)
  Pallas kernels: 136 us -> 127 us
  other arithmetic: 2.72 us -> 0 us
    pallas_call x1, Pallas kernels: 136 us -> 127 us  [local_run(): pl.pallas_call(functools.partial(kernel, nb, rank, base_eta), out_shape=(...]
    select_n x1 -> x0, other arithmetic: 2.72 us -> none  [local_run(): coded = jnp.where(mask_loc != 0, rate_loc, jnp.inf)]
    unnamed x5 -> x2, local copies, waits for them, and re-layouts: 4.29 us -> 2.91 us
where the time goes in v2:
time: 131 us
  Pallas kernels  127 us (97%)
  local copies, waits for them, and re-layouts  2.91 us (2%)
    pallas_call x1, Pallas kernels, local_run(): pl.pallas_call(functools.partial(kernel, nb, rank, base_eta), out_shape=(...  127 us
    unnamed x2, local copies, waits for them, and re-layouts  2.91 us

profile of v2, /device:TPU:1, one launch (start us, length us, event | category | flops | bytes accessed | tf_op | source)
XLA Modules:
  0.0 130.6 jit_solution(6980188332425770769)
XLA Ops:
  0.6 127.0 %dsgd.1 = (f32[50,128]{1,0:T(8,128)}, f32[50,512]{1,0:T(8,128)}) custom-call(f32[4,64]{1,0:T(4,128)} %bitcast.9, f32[512,512]{1,0:T(8,128)} %rate.1, s32[512,512]{1,0:T(8,128)} %mask.1, f32[50,128]{1,0:T(8,128)} %bitcast.7, f32[50,512]{1,0:T(8,128)} %bitcast.6), custom_call_target="tpu_custom_call" | custom-call | tf_op jit(solution)/shard_map/dsgd/pallas_call | solution.py:240
  127.6 1.4 %copy.9 = f32[128,50]{0,1:T(8,128)} copy(f32[128,50]{0,1:T(8,128)} %bitcast.8) | data formatting | bytes 51200
  129.0 1.6 %copy.10 = f32[512,50]{0,1:T(8,128)} copy(f32[512,50]{0,1:T(8,128)} %bitcast.5) | data formatting | bytes 204800

commit v3 on v2

--- a/solution.py
+++ b/solution.py
@@ -10,7 +10,6 @@
 from jax.sharding import PartitionSpec as P
 
 LAMBDA = 0.05
-LEADER = 1
 STEPS = 4
 KPAD = 64
 UNROLL = 12
@@ -78,9 +77,18 @@
 
 
 def kernel(nb, rank, base_eta, lr, rate, mask, ut_in, vt_in, ut_out, vt_out,
-           r_all, m_all, r_own, m_own, ut_land, vt_land, u32, v32, ub, utb, vb,
-           rl_sem, ml_sem, r_sem, s_sem, u_sem, v_sem, us_sem, vs_sem, ou_sem, ov_sem, ous_sem, ovs_sem):
+           r_all, m_all, r_own, m_own, hop_1, hop_2, ut_land, vt_land, u32, v32, ub, utb, vb,
+           rl_sem, ml_sem, r_sem, s_sem, u_sem, v_sem, us_sem, vs_sem, ou_sem, ov_sem, ous_sem, ovs_sem,
+           h1_sem, h1s_sem, h2_sem, h2s_sem, h3_sem, h3s_sem):
     me = lax.axis_index("blk")
+    rep = lax.axis_index("rep")
+    other = 1 - rep
+    lead = 2 * rep + 1
+    mate = 2 * rep
+    far_0 = lax.rem(lead + 1, nb)
+    far_1 = lax.rem(lead + 2, nb)
+    late = nb - 1
+    parts = hop_1.shape[1]
     rows, cols = r_all.shape[2:]
     subs = lr.shape[1]
     half = cols // 2
@@ -98,55 +106,125 @@
         for cp in pair:
             cp.start()
 
-    @pl.when(me != LEADER)
+    def device(r, b):
+        return dict(device_id={"rep": r, "blk": b}, device_id_type=MESH_ID)
+
+    def tell(*who):
+        for r, b in who:
+            pl.semaphore_signal(barrier, inc=1, **device(r, b))
+
+    def encode(w):
+        for cp in loads[w]:
+            cp.wait()
+        r_own[w] = jnp.where(m_own[w] != 0, r_own[w], jnp.inf)
+
+    def send_factors():
+        cps = [
+            pltpu.make_async_remote_copy(ut_in, ut_land.at[me], us_sem, u_sem.at[me], **device(rep, lead)),
+            pltpu.make_async_remote_copy(vt_in, vt_land.at[me], vs_sem, v_sem.at[me], **device(rep, lead)),
+        ]
+        for cp in cps:
+            cp.start()
+        return cps
+
+    def send_block(w):
+        cp = pltpu.make_async_remote_copy(
+            r_own.at[w], r_all.at[w, me], s_sem.at[w], r_sem.at[w, me], **device(rep, lead)
+        )
+        cp.start()
+        return cp
+
+    def get_results():
+        pltpu.make_async_copy(ut_out, ut_out, ou_sem).wait()
+        pltpu.make_async_copy(vt_out, vt_out, ov_sem).wait()
+
+    def finish(cps):
+        for cp in cps:
+            cp.wait_send()
+        get_results()
+
+    def part_rows(c):
+        return pl.ds(c * hop_1.shape[2], hop_1.shape[2])
+
+    def send_far(side):
+        cps = send_factors()
+        cps.append(send_block(0))
+        for c in range(parts):
+            cps.append(pltpu.make_async_remote_copy(
+                r_own.at[late, part_rows(c)], hop_1.at[side, c], h1s_sem.at[c], h1_sem.at[side, c],
+                **device(other, 2 * other),
+            ))
+            cps[-1].start()
+        for w in range(1, late):
+            encode(w)
+        for w in range(1, late):
+            cps.append(send_block(w))
+        return cps
+
+    @pl.when(me == far_0)
     def _():
-        to = dict(device_id={"blk": LEADER}, device_id_type=MESH_ID)
-        pl.semaphore_signal(barrier, inc=1, **to)
-
-        def encode(w):
-            for cp in loads[w]:
-                cp.wait()
-            r_own[w] = jnp.where(m_own[w] != 0, r_own[w], jnp.inf)
-
+        tell((rep, lead))
+        encode(0)
+        encode(late)
+        pl.semaphore_wait(barrier, 2)
+        finish(send_far(0))
+
+    @pl.when(me == far_1)
+    def _():
+        tell((rep, lead), (rep, mate))
+        encode(0)
+        encode(late)
+        pl.semaphore_wait(barrier, 3)
+        cps = send_far(1)
+        for c in range(parts):
+            for side in range(2):
+                pltpu.make_async_copy(hop_2.at[side, c], hop_2.at[side, c], h2_sem.at[side, c]).wait()
+                home = lax.rem(2 * other + 2 + side, nb)
+                cps.append(pltpu.make_async_remote_copy(
+                    hop_2.at[side, c], r_all.at[late, home, part_rows(c)], h3s_sem.at[side, c], h3_sem.at[side, c],
+                    **device(other, 2 * other + 1),
+                ))
+                cps[-1].start()
+        finish(cps)
+
+    @pl.when(me == mate)
+    def _():
+        tell((rep, lead), (other, lax.rem(2 * other + 2, nb)), (other, lax.rem(2 * other + 3, nb)))
         encode(0)
         encode(1)
-        pl.semaphore_wait(barrier, 1)
-        cps = [
-            pltpu.make_async_remote_copy(ut_in, ut_land.at[me], us_sem, u_sem.at[me], **to),
-            pltpu.make_async_remote_copy(vt_in, vt_land.at[me], vs_sem, v_sem.at[me], **to),
-        ]
-        for w in range(nb):
-            cps.append(pltpu.make_async_remote_copy(r_own.at[w], r_all.at[w, me], s_sem.at[w], r_sem.at[w, me], **to))
-        for cp in cps[:3]:
-            cp.start()
-        encode(2)
-        cps[3].start()
-        encode(3)
-        for cp in cps[4:]:
-            cp.start()
-        for cp in cps:
-            cp.wait_send()
-        pltpu.make_async_copy(ut_out, ut_out, ou_sem).wait()
-        pltpu.make_async_copy(vt_out, vt_out, ov_sem).wait()
-
-    @pl.when(me == LEADER)
+        pl.semaphore_wait(barrier, 2)
+        cps = send_factors()
+        cps.append(send_block(0))
+        for w in range(2, nb):
+            encode(w)
+        for w in range(1, nb):
+            cps.append(send_block(w))
+        for c in range(parts):
+            for side in range(2):
+                pltpu.make_async_copy(hop_1.at[side, c], hop_1.at[side, c], h1_sem.at[side, c]).wait()
+                cps.append(pltpu.make_async_remote_copy(
+                    hop_1.at[side, c], hop_2.at[side, c], h2s_sem.at[side, c], h2_sem.at[side, c],
+                    **device(rep, far_1),
+                ))
+                cps[-1].start()
+        finish(cps)
+
+    @pl.when(me == lead)
     def _():
-        others = [j for j in range(nb) if j != LEADER]
-        for j in others:
-            pl.semaphore_signal(barrier, inc=1, device_id={"blk": j}, device_id_type=MESH_ID)
-        ut_land[LEADER] = ut_in[...]
-        vt_land[LEADER] = vt_in[...]
+        tell((rep, mate), (rep, far_0), (rep, far_1), (other, lax.rem(2 * other + 3, nb)))
+        ut_land[lead] = ut_in[...]
+        vt_land[lead] = vt_in[...]
         for w in range(nb):
             for cp in loads[w]:
                 cp.wait()
-            m_all[w, LEADER] = m_own[w].astype(F32).astype(BF16)
-            r_all[w, LEADER] = r_own[w]
+            m_all[w, lead] = m_own[w].astype(F32).astype(BF16)
+            r_all[w, lead] = r_own[w]
         pl.semaphore_wait(barrier, nb - 1)
 
+        for b in (mate, far_0, far_1):
+            pltpu.make_async_copy(ut_land.at[b], ut_land.at[b], u_sem.at[b]).wait()
+            pltpu.make_async_copy(vt_land.at[b], vt_land.at[b], v_sem.at[b]).wait()
         for i in range(nb):
-            if i != LEADER:
-                pltpu.make_async_copy(ut_land.at[i], ut_land.at[i], u_sem.at[i]).wait()
-                pltpu.make_async_copy(vt_land.at[i], vt_land.at[i], v_sem.at[i]).wait()
             v32[i] = jnp.zeros(v32.shape[1:], F32)
             v32[i, :rank] = vt_land[i]
             vb[i] = v32[i].astype(BF16)
@@ -187,8 +265,21 @@
         order_n = make_order(nb, UNROLL, 0)
 
         def first_epoch(w, carry):
-            for j in [j for j in range(nb) if j != LEADER]:
-                pltpu.make_async_copy(r_all.at[w, j], r_all.at[w, j], r_sem.at[w, j]).wait()
+            pltpu.make_async_copy(r_all.at[w, mate], r_all.at[w, mate], r_sem.at[w, mate]).wait()
+
+            @pl.when(w < late)
+            def _():
+                for j in (far_0, far_1):
+                    pltpu.make_async_copy(r_all.at[w, j], r_all.at[w, j], r_sem.at[w, j]).wait()
+
+            @pl.when(w == late)
+            def _():
+                for c in range(parts):
+                    for side, j in enumerate((far_0, far_1)):
+                        dst = r_all.at[late, j, part_rows(c)]
+                        pltpu.make_async_copy(dst, dst, h3_sem.at[side, c]).wait()
+
+            for j in (mate, far_0, far_1):
                 coded = r_all[w, j]
                 seen = coded < jnp.inf
                 m_all[w, j] = jnp.where(seen, 1.0, 0.0).astype(BF16)
@@ -208,16 +299,16 @@
             ut_land[i] = ut[:rank]
             vt_land[i] = v32[i, :rank]
         cps = []
-        for n, j in enumerate(others):
-            to = dict(device_id={"blk": j}, device_id_type=MESH_ID)
+        for n, j in enumerate((mate, far_0, far_1)):
+            to = device(rep, j)
             cps.append(pltpu.make_async_remote_copy(vt_land.at[j], vt_out, ovs_sem.at[n], ov_sem, **to))
             cps.append(pltpu.make_async_remote_copy(ut_land.at[j], ut_out, ous_sem.at[n], ou_sem, **to))
         cps.reverse()
         for cp in cps:
             cp.start()
         mine = [
-            pltpu.make_async_copy(ut_land.at[LEADER], ut_out, ou_sem),
-            pltpu.make_async_copy(vt_land.at[LEADER], vt_out, ov_sem),
+            pltpu.make_async_copy(ut_land.at[lead], ut_out, ou_sem),
+            pltpu.make_async_copy(vt_land.at[lead], vt_out, ov_sem),
         ]
         for cp in mine:
             cp.start()
@@ -247,6 +338,8 @@
                 pltpu.VMEM((nb, nb, rows, cols), BF16),
                 pltpu.VMEM((nb, rows, cols), F32),
                 pltpu.VMEM((nb, rows, cols), jnp.int32),
+                pltpu.VMEM((2, 4, rows // 4, cols), F32),
+                pltpu.VMEM((2, 4, rows // 4, cols), F32),
                 pltpu.VMEM((nb, rank, rows), F32),
                 pltpu.VMEM((nb, rank, cols), F32),
                 pltpu.VMEM((nb, rows, KPAD), F32),
@@ -257,6 +350,7 @@
                 dma((nb,)), dma((nb,)),
                 dma((nb, nb)), dma((nb,)), dma((nb,)), dma((nb,)), dma, dma,
                 dma, dma, dma((nb - 1,)), dma((nb - 1,)),
+                dma((2, 4)), dma((4,)), dma((2, 4)), dma((2, 4)), dma((2, 4)), dma((2, 4)),
             ],
             compiler_params=pltpu.CompilerParams(collective_id=0, has_side_effects=True),
             name="dsgd",

time: 131 us -> 128 us (0.977)
  Pallas kernels: 127 us -> 125 us
    pallas_call x1, Pallas kernels: 127 us -> 125 us  [local_run(): pl.pallas_call(functools.partial(kernel, nb, rank, base_eta), out_shape=(...]
where the time goes in v3:
time: 128 us
  Pallas kernels  125 us (98%)
  local copies, waits for them, and re-layouts  2.91 us (2%)
    pallas_call x1, Pallas kernels, local_run(): pl.pallas_call(functools.partial(kernel, nb, rank, base_eta), out_shape=(...  125 us
    unnamed x2, local copies, waits for them, and re-layouts  2.91 us

profile of v3, /device:TPU:1, one launch (start us, length us, event | category | flops | bytes accessed | tf_op | source)
XLA Modules:
  0.0 128.1 jit_solution(15315159158335586953)
XLA Ops:
  0.6 124.6 %dsgd.1 = (f32[50,128]{1,0:T(8,128)}, f32[50,512]{1,0:T(8,128)}) custom-call(f32[4,64]{1,0:T(4,128)} %bitcast.9, f32[512,512]{1,0:T(8,128)} %rate.1, s32[512,512]{1,0:T(8,128)} %mask.1, f32[50,128]{1,0:T(8,128)} %bitcast.7, f32[50,512]{1,0:T(8,128)} %bitcast.6), custom_call_target="tpu_custom_call" | custom-call | tf_op jit(solution)/shard_map/dsgd/pallas_call | solution.py:331
  125.2 1.4 %copy.9 = f32[128,50]{0,1:T(8,128)} copy(f32[128,50]{0,1:T(8,128)} %bitcast.8) | data formatting | bytes 51200
  126.6 1.6 %copy.10 = f32[512,50]{0,1:T(8,128)} copy(f32[512,50]{0,1:T(8,128)} %bitcast.5) | data formatting | bytes 204800

commit v4 on v3

--- a/solution.py
+++ b/solution.py
@@ -13,7 +13,7 @@
 STEPS = 4
 KPAD = 64
 UNROLL = 12
-LEN_A, LEN_B, A_TO_B, B_TO_C, LEN_C = 64, 96, 226, 211, 80
+LEN_A, LEN_B, A_TO_B, B_TO_C, LEN_C = 64, 96, 226, 211, 35
 F32 = jnp.float32
 BF16 = jnp.bfloat16
 MESH_ID = pl.DeviceIdType.MESH
@@ -22,39 +22,44 @@
 def play(order, nb):
     now, start, done = 0, {}, {}
     for kind, s, i in order:
-        if kind == "A":
+        if kind == 0:
             ready = 0
             if s > 0:
                 before = [(s - 1, i)] + ([(s - 1, (i - 1) % nb)] if s % STEPS == 0 else [])
                 if any(d not in done for d in before):
                     return None
                 ready = max(done[d] for d in before)
-            start[kind, s, i] = max(now, ready)
-            now = start[kind, s, i] + LEN_A
+            now = max(now, ready)
+            start[kind, s, i] = now
+            now += LEN_A
         else:
-            if ("A", s, i) not in start:
+            if (0, s, i) not in start:
                 return None
-            start[kind, s, i] = max(now, start["A", s, i] + A_TO_B)
-            now = start[kind, s, i] + LEN_B
+            now = max(now, start[0, s, i] + A_TO_B)
+            start[kind, s, i] = now
+            now += LEN_B
             done[s, i] = now + B_TO_C + LEN_C
-    return max(done.values()), start
-
-
-def make_order(nb, subs, tries):
-    users = [(s, i) for s in range(STEPS * subs) for i in reversed(range(nb))]
-    best = []
-    for n in range(len(users) + 1):
-        best += [("A", *users[n])] if n < len(users) else []
-        best += [("B", *users[n - 1])] if n > 0 else []
-    rnd = random.Random(0)
-    cur, length = best, play(best, nb)[0]
-    low = length
+    return now, start
+
+
+def repeat(place, nb, subs):
+    keys = [(t + u * 2 * STEPS * nb, kind, s + u * STEPS, i) for u in range(subs) for (kind, s, i), t in place.items()]
+    return [k[1:] for k in sorted(keys)]
+
+
+def find_places(nb, tries, seed):
+    place = {}
+    for n in range(STEPS * nb):
+        s, i = n // nb, nb - 1 - n % nb
+        place[0, s, i], place[1, s, i] = 2.0 * n, 2.0 * n + 3.0
+    rnd = random.Random(seed)
+    names = list(place)
+    cur = best = place
+    length = low = play(repeat(place, nb, 5), nb)[0]
     for it in range(tries):
-        new = list(cur)
-        at = rnd.randrange(len(new))
-        item = new.pop(at)
-        new.insert(max(0, at + rnd.choice((-4, -3, -2, -1, 1, 2, 3, 4))), item)
-        played = play(new, nb)
+        new = dict(cur)
+        new[rnd.choice(names)] += rnd.choice((-4.5, -3.5, -2.5, -1.5, 1.5, 2.5, 3.5, 4.5)) + rnd.uniform(-0.2, 0.2)
+        played = play(repeat(new, nb, 5), nb)
         if played is None:
             continue
         temp = 60 * (1 - it / tries) + 0.5
@@ -62,9 +67,13 @@
             cur, length = new, played[0]
             if length < low:
                 best, low = new, length
-    start = play(best, nb)[1]
-    events = [(t, 1, *key) for key, t in start.items()]
-    events += [(t + LEN_B + B_TO_C, 0, "C", s, i) for (kind, s, i), t in start.items() if kind == "B"]
+    return best
+
+
+def make_order(place, nb, subs):
+    start = play(repeat(place, nb, subs), nb)[1]
+    events = [(t, 1, "AB"[key[0]], *key[1:]) for key, t in start.items()]
+    events += [(t + LEN_B + B_TO_C, 0, "C", *key[1:]) for key, t in start.items() if key[0] == 1]
     return [e[2:] for e in sorted(events)]
 
 
@@ -87,7 +96,8 @@
     mate = 2 * rep
     far_0 = lax.rem(lead + 1, nb)
     far_1 = lax.rem(lead + 2, nb)
-    late = nb - 1
+    late = nb - 2
+    direct = [w for w in range(nb) if w != late]
     parts = hop_1.shape[1]
     rows, cols = r_all.shape[2:]
     subs = lr.shape[1]
@@ -155,9 +165,9 @@
                 **device(other, 2 * other),
             ))
             cps[-1].start()
-        for w in range(1, late):
+        for w in direct[1:]:
             encode(w)
-        for w in range(1, late):
+        for w in direct[1:]:
             cps.append(send_block(w))
         return cps
 
@@ -261,13 +271,14 @@
                         v32[j, :, h] = v_new
                         vb[j, :, h] = v_new.astype(BF16)
 
-        order_1 = make_order(nb, 1, 3000)
-        order_n = make_order(nb, UNROLL, 0)
+        place = find_places(nb, 12000, 1)
+        order_1 = make_order(place, nb, 1)
+        order_n = make_order(place, nb, UNROLL)
 
         def first_epoch(w, carry):
             pltpu.make_async_copy(r_all.at[w, mate], r_all.at[w, mate], r_sem.at[w, mate]).wait()
 
-            @pl.when(w < late)
+            @pl.when(w != late)
             def _():
                 for j in (far_0, far_1):
                     pltpu.make_async_copy(r_all.at[w, j], r_all.at[w, j], r_sem.at[w, j]).wait()

time: 128 us -> 126 us (0.984)
  Pallas kernels: 125 us -> 122 us
    pallas_call x1, Pallas kernels: 125 us -> 122 us  [local_run(): pl.pallas_call(functools.partial(kernel, nb, rank, base_eta), out_shape=(...]
where the time goes in v4:
time: 126 us
  Pallas kernels  122 us (97%)
  local copies, waits for them, and re-layouts  2.91 us (2%)
    pallas_call x1, Pallas kernels, local_run(): pl.pallas_call(functools.partial(kernel, nb, rank, base_eta), out_shape=(...  122 us
    unnamed x2, local copies, waits for them, and re-layouts  2.91 us

profile of v4, /device:TPU:1, one launch (start us, length us, event | category | flops | bytes accessed | tf_op | source)
XLA Modules:
  0.0 125.9 jit_solution(12601403293780863795)
XLA Ops:
  0.6 122.3 %dsgd.1 = (f32[50,128]{1,0:T(8,128)}, f32[50,512]{1,0:T(8,128)}) custom-call(f32[4,64]{1,0:T(4,128)} %bitcast.9, f32[512,512]{1,0:T(8,128)} %rate.1, s32[512,512]{1,0:T(8,128)} %mask.1, f32[50,128]{1,0:T(8,128)} %bitcast.7, f32[50,512]{1,0:T(8,128)} %bitcast.6), custom_call_target="tpu_custom_call" | custom-call | tf_op jit(solution)/shard_map/dsgd/pallas_call | solution.py:342
  123.0 1.4 %copy.9 = f32[128,50]{0,1:T(8,128)} copy(f32[128,50]{0,1:T(8,128)} %bitcast.8) | data formatting | bytes 51200
  124.3 1.6 %copy.10 = f32[512,50]{0,1:T(8,128)} copy(f32[512,50]{0,1:T(8,128)} %bitcast.5) | data formatting | bytes 204800

commit v5 on v4

--- a/solution.py
+++ b/solution.py
@@ -337,13 +337,14 @@
         cols = item_loc.shape[0]
         base_eta = math.sqrt(rank) / (4.0 * (cols + 2 * rank))
         vmem = pl.BlockSpec(memory_space=pltpu.VMEM)
-        hbm = pl.BlockSpec(memory_space=pl.ANY)
+        hbm = pl.BlockSpec(memory_space=pltpu.HBM)
+        anywhere = pl.BlockSpec(memory_space=pl.ANY)
         dma = pltpu.SemaphoreType.DMA
         ut, vt = pl.pallas_call(
             functools.partial(kernel, nb, rank, base_eta),
             out_shape=(jax.ShapeDtypeStruct((rank, rows), F32), jax.ShapeDtypeStruct((rank, cols), F32)),
             in_specs=[pl.BlockSpec(memory_space=pltpu.SMEM), hbm, hbm, vmem, vmem],
-            out_specs=(hbm, hbm),
+            out_specs=(anywhere, anywhere),
             scratch_shapes=[
                 pltpu.VMEM((nb, nb, rows, cols), F32),
                 pltpu.VMEM((nb, nb, rows, cols), BF16),
@@ -363,7 +364,7 @@
                 dma, dma, dma((nb - 1,)), dma((nb - 1,)),
                 dma((2, 4)), dma((4,)), dma((2, 4)), dma((2, 4)), dma((2, 4)), dma((2, 4)),
             ],
-            compiler_params=pltpu.CompilerParams(collective_id=0, has_side_effects=True),
+            compiler_params=pltpu.CompilerParams(collective_id=0, has_side_effects=True, vmem_limit_bytes=53 * 2**20),
             name="dsgd",
         )(lr_scale.T, rate_loc, mask_loc, user_loc.T, item_loc.T)
         return ut.T, vt.T

time: 126 us -> 126 us (level)
    unnamed x2 -> x8, local copies, waits for them, and re-layouts: 2.91 us -> 3.58 us
where the time goes in v5:
time: 126 us
  Pallas kernels  122 us (97%)
  local copies, waits for them, and re-layouts  3.58 us (3%)
    pallas_call x1, Pallas kernels, local_run(): pl.pallas_call(functools.partial(kernel, nb, rank, base_eta), out_shape=(...  122 us
    unnamed x8, local copies, waits for them, and re-layouts  3.58 us

profile of v5, /device:TPU:1, one launch (start us, length us, event | category | flops | bytes accessed | tf_op | source)
XLA Modules:
  0.0 126.2 jit_solution(3894898325500789823)
XLA Ops:
  0.6 0.0 copy-start.2
  0.6 0.7 copy-done.2
  1.3 0.0 copy-start
  1.3 0.9 copy-done
  2.2 0.0 copy-start.1
  2.2 0.7 copy-done.1
  3.0 122.0 %dsgd.1 = (f32[50,128]{1,0:T(8,128)S(1)}, f32[50,512]{1,0:T(8,128)S(1)}) custom-call(f32[4,64]{1,0:T(4,128)S(1)} %bitcast.9, f32[512,512]{1,0:T(8,128)} %rate.1, s32[512,512]{1,0:T(8,128)} %mask.1, f32[50,128]{1,0:T(8,128)S(1)} %bitcast.7, f32[50,512]{1,0:T(8,128)S(1)} %bitcast.6), custom_call_target="tpu_custom_call" | custom-call | tf_op jit(solution)/shard_map/dsgd/pallas_call | solution.py:343
  125.0 0.6 copy.9
  125.6 0.6 copy.10
Async XLA Ops:
  0.6 0.7 copy-start.2
  1.3 0.9 copy-start
  2.2 0.7 copy-start.1

commit v6 on v4

--- a/solution.py
+++ b/solution.py
@@ -85,10 +85,10 @@
     return lax.dot_general(a, b, (((1,), (1,)), ((), ())), preferred_element_type=F32)
 
 
-def kernel(nb, rank, base_eta, lr, rate, mask, ut_in, vt_in, ut_out, vt_out,
+def kernel(nb, rank, base_eta, lr_in, rate, mask, ut_in, vt_in, ut_out, vt_out,
            r_all, m_all, r_own, m_own, hop_1, hop_2, ut_land, vt_land, u32, v32, ub, utb, vb,
            rl_sem, ml_sem, r_sem, s_sem, u_sem, v_sem, us_sem, vs_sem, ou_sem, ov_sem, ous_sem, ovs_sem,
-           h1_sem, h1s_sem, h2_sem, h2s_sem, h3_sem, h3s_sem):
+           lr, lr_sem, h1_sem, h1s_sem, h2_sem, h2s_sem, h3_sem, h3s_sem):
     me = lax.axis_index("blk")
     rep = lax.axis_index("rep")
     other = 1 - rep
@@ -222,13 +222,20 @@
     @pl.when(me == lead)
     def _():
         tell((rep, mate), (rep, far_0), (rep, far_1), (other, lax.rem(2 * other + 3, nb)))
-        ut_land[lead] = ut_in[...]
-        vt_land[lead] = vt_in[...]
+        own = [
+            pltpu.make_async_copy(ut_in, ut_land.at[lead], us_sem),
+            pltpu.make_async_copy(vt_in, vt_land.at[lead], vs_sem),
+            pltpu.make_async_copy(lr_in, lr, lr_sem),
+        ]
+        for cp in own:
+            cp.start()
         for w in range(nb):
             for cp in loads[w]:
                 cp.wait()
             m_all[w, lead] = m_own[w].astype(F32).astype(BF16)
             r_all[w, lead] = r_own[w]
+        for cp in own:
+            cp.wait()
         pl.semaphore_wait(barrier, nb - 1)
 
         for b in (mate, far_0, far_1):
@@ -305,26 +312,24 @@
         lax.fori_loop(0, nb, first_epoch, 0)
         lax.fori_loop(0, (subs - nb) // UNROLL, later, 0)
 
-        for i in range(nb):
-            ut = jnp.concatenate([u32[i], jnp.zeros((rows, rows - KPAD), F32)], axis=1).T
-            ut_land[i] = ut[:rank]
-            vt_land[i] = v32[i, :rank]
+        def stage(j):
+            vt_land[j] = v32[j, :rank]
+            ut_land[j] = jnp.concatenate([u32[j], jnp.zeros((rows, rows - KPAD), F32)], axis=1).T[:rank]
+
+        def send_home(n, j):
+            for src, dst, s_out, s_in in ((vt_land, vt_out, ovs_sem, ov_sem), (ut_land, ut_out, ous_sem, ou_sem)):
+                cps.append(pltpu.make_async_remote_copy(src.at[j], dst, s_out.at[n], s_in, **device(rep, j)))
+                cps[-1].start()
+
         cps = []
-        for n, j in enumerate((mate, far_0, far_1)):
-            to = device(rep, j)
-            cps.append(pltpu.make_async_remote_copy(vt_land.at[j], vt_out, ovs_sem.at[n], ov_sem, **to))
-            cps.append(pltpu.make_async_remote_copy(ut_land.at[j], ut_out, ous_sem.at[n], ou_sem, **to))
-        cps.reverse()
-        for cp in cps:
-            cp.start()
-        mine = [
-            pltpu.make_async_copy(ut_land.at[lead], ut_out, ou_sem),
-            pltpu.make_async_copy(vt_land.at[lead], vt_out, ov_sem),
-        ]
-        for cp in mine:
-            cp.start()
-        for cp in mine:
-            cp.wait()
+        stage(far_0)
+        stage(far_1)
+        send_home(0, far_0)
+        send_home(1, far_1)
+        stage(mate)
+        vt_out[...] = v32[lead, :rank]
+        send_home(2, mate)
+        ut_out[...] = jnp.concatenate([u32[lead], jnp.zeros((rows, rows - KPAD), F32)], axis=1).T[:rank]
         for cp in cps:
             cp.wait_send()
 
@@ -335,15 +340,15 @@
     def local_run(rate_loc, mask_loc, user_loc, item_loc, lr_scale):
         rows, rank = user_loc.shape
         cols = item_loc.shape[0]
+        subs = lr_scale.shape[0]
         base_eta = math.sqrt(rank) / (4.0 * (cols + 2 * rank))
-        vmem = pl.BlockSpec(memory_space=pltpu.VMEM)
-        hbm = pl.BlockSpec(memory_space=pl.ANY)
+        anywhere = pl.BlockSpec(memory_space=pl.ANY)
         dma = pltpu.SemaphoreType.DMA
         ut, vt = pl.pallas_call(
             functools.partial(kernel, nb, rank, base_eta),
-            out_shape=(jax.ShapeDtypeStruct((rank, rows), F32), jax.ShapeDtypeStruct((rank, cols), F32)),
-            in_specs=[pl.BlockSpec(memory_space=pltpu.SMEM), hbm, hbm, vmem, vmem],
-            out_specs=(hbm, hbm),
+            out_shape=(pltpu.VMEM((rank, rows), F32), pltpu.VMEM((rank, cols), F32)),
+            in_specs=[anywhere] * 5,
+            out_specs=(pl.BlockSpec(memory_space=pltpu.VMEM),) * 2,
             scratch_shapes=[
                 pltpu.VMEM((nb, nb, rows, cols), F32),
                 pltpu.VMEM((nb, nb, rows, cols), BF16),
@@ -361,6 +366,7 @@
                 dma((nb,)), dma((nb,)),
                 dma((nb, nb)), dma((nb,)), dma((nb,)), dma((nb,)), dma, dma,
                 dma, dma, dma((nb - 1,)), dma((nb - 1,)),
+                pltpu.SMEM((STEPS, subs), F32), dma,
                 dma((2, 4)), dma((4,)), dma((2, 4)), dma((2, 4)), dma((2, 4)), dma((2, 4)),
             ],
             compiler_params=pltpu.CompilerParams(collective_id=0, has_side_effects=True),

time: 126 us -> 123 us (0.976)
  local copies, waits for them, and re-layouts: 2.91 us -> 1.26 us
    unnamed x2, local copies, waits for them, and re-layouts: 2.91 us -> 1.26 us
    pallas_call x1, Pallas kernels: 122 us -> 121 us  [local_run(): pl.pallas_call(functools.partial(kernel, nb, rank, base_eta), out_shape=(...]
where the time goes in v6:
time: 123 us
  Pallas kernels  121 us (98%)
  local copies, waits for them, and re-layouts  1.26 us (1%)
    pallas_call x1, Pallas kernels, local_run(): pl.pallas_call(functools.partial(kernel, nb, rank, base_eta), out_shape=(...  121 us

profile of v6, /device:TPU:1, one launch (start us, length us, event | category | flops | bytes accessed | tf_op | source)
XLA Modules:
  0.0 122.9 jit_solution(17807170326996023434)
XLA Ops:
  0.6 121.0 %dsgd.1 = (f32[50,128]{1,0:T(8,128)S(1)}, f32[50,512]{1,0:T(8,128)S(1)}) custom-call(f32[4,64]{1,0:T(4,128)} %bitcast.9, f32[512,512]{1,0:T(8,128)} %rate.1, s32[512,512]{1,0:T(8,128)} %mask.1, f32[50,128]{1,0:T(8,128)} %bitcast.8, f32[50,512]{1,0:T(8,128)} %bitcast.7), custom_call_target="tpu_custom_call" | custom-call | tf_op jit(solution)/shard_map/dsgd/pallas_call | solution.py:347
  121.7 0.6 copy.9
  122.3 0.6 copy.10

commit v7 on v6

--- a/solution.py
+++ b/solution.py
@@ -86,9 +86,9 @@
 
 
 def kernel(nb, rank, base_eta, lr_in, rate, mask, ut_in, vt_in, ut_out, vt_out,
-           r_all, m_all, r_own, m_own, hop_1, hop_2, ut_land, vt_land, u32, v32, ub, utb, vb,
+           r_all, m_all, r_own, m_own, hop_1, ut_land, vt_land, u32, v32, ub, utb, vb,
            rl_sem, ml_sem, r_sem, s_sem, u_sem, v_sem, us_sem, vs_sem, ou_sem, ov_sem, ous_sem, ovs_sem,
-           lr, lr_sem, h1_sem, h1s_sem, h2_sem, h2s_sem, h3_sem, h3s_sem):
+           lr, lr_sem, h1_sem, h1s_sem, h2s_sem, h3_sem):
     me = lax.axis_index("blk")
     rep = lax.axis_index("rep")
     other = 1 - rep
@@ -181,21 +181,11 @@
 
     @pl.when(me == far_1)
     def _():
-        tell((rep, lead), (rep, mate))
+        tell((rep, lead))
         encode(0)
         encode(late)
-        pl.semaphore_wait(barrier, 3)
-        cps = send_far(1)
-        for c in range(parts):
-            for side in range(2):
-                pltpu.make_async_copy(hop_2.at[side, c], hop_2.at[side, c], h2_sem.at[side, c]).wait()
-                home = lax.rem(2 * other + 2 + side, nb)
-                cps.append(pltpu.make_async_remote_copy(
-                    hop_2.at[side, c], r_all.at[late, home, part_rows(c)], h3s_sem.at[side, c], h3_sem.at[side, c],
-                    **device(other, 2 * other + 1),
-                ))
-                cps[-1].start()
-        finish(cps)
+        pl.semaphore_wait(barrier, 2)
+        finish(send_far(1))
 
     @pl.when(me == mate)
     def _():
@@ -212,16 +202,17 @@
         for c in range(parts):
             for side in range(2):
                 pltpu.make_async_copy(hop_1.at[side, c], hop_1.at[side, c], h1_sem.at[side, c]).wait()
+                home = lax.rem(2 * other + 2 + side, nb)
                 cps.append(pltpu.make_async_remote_copy(
-                    hop_1.at[side, c], hop_2.at[side, c], h2s_sem.at[side, c], h2_sem.at[side, c],
-                    **device(rep, far_1),
+                    hop_1.at[side, c], r_all.at[late, home, part_rows(c)], h2s_sem.at[side, c], h3_sem.at[side, c],
+                    **device(other, 2 * other + 1),
                 ))
                 cps[-1].start()
         finish(cps)
 
     @pl.when(me == lead)
     def _():
-        tell((rep, mate), (rep, far_0), (rep, far_1), (other, lax.rem(2 * other + 3, nb)))
+        tell((rep, mate), (rep, far_0), (rep, far_1), (other, 2 * other))
         own = [
             pltpu.make_async_copy(ut_in, ut_land.at[lead], us_sem),
             pltpu.make_async_copy(vt_in, vt_land.at[lead], vs_sem),
@@ -355,7 +346,6 @@
                 pltpu.VMEM((nb, rows, cols), F32),
                 pltpu.VMEM((nb, rows, cols), jnp.int32),
                 pltpu.VMEM((2, 4, rows // 4, cols), F32),
-                pltpu.VMEM((2, 4, rows // 4, cols), F32),
                 pltpu.VMEM((nb, rank, rows), F32),
                 pltpu.VMEM((nb, rank, cols), F32),
                 pltpu.VMEM((nb, rows, KPAD), F32),
@@ -367,7 +357,7 @@
                 dma((nb, nb)), dma((nb,)), dma((nb,)), dma((nb,)), dma, dma,
                 dma, dma, dma((nb - 1,)), dma((nb - 1,)),
                 pltpu.SMEM((STEPS, subs), F32), dma,
-                dma((2, 4)), dma((4,)), dma((2, 4)), dma((2, 4)), dma((2, 4)), dma((2, 4)),
+                dma((2, 4)), dma((4,)), dma((2, 4)), dma((2, 4)),
             ],
             compiler_params=pltpu.CompilerParams(collective_id=0, has_side_effects=True),
             name="dsgd",

time: 123 us -> 123 us (level)
  no operation moved by 1% of the time
where the time goes in v7:
time: 123 us
  Pallas kernels  121 us (98%)
  local copies, waits for them, and re-layouts  1.26 us (1%)
    pallas_call x1, Pallas kernels, local_run(): pl.pallas_call(functools.partial(kernel, nb, rank, base_eta), out_shape=(...  121 us

profile of v7, /device:TPU:1, one launch (start us, length us, event | category | flops | bytes accessed | tf_op | source)
XLA Modules:
  0.0 122.8 jit_solution(16241386509957279380)
XLA Ops:
  0.6 120.9 %dsgd.1 = (f32[50,128]{1,0:T(8,128)S(1)}, f32[50,512]{1,0:T(8,128)S(1)}) custom-call(f32[4,64]{1,0:T(4,128)} %bitcast.9, f32[512,512]{1,0:T(8,128)} %rate.1, s32[512,512]{1,0:T(8,128)} %mask.1, f32[50,128]{1,0:T(8,128)} %bitcast.8, f32[50,512]{1,0:T(8,128)} %bitcast.7), custom_call_target="tpu_custom_call" | custom-call | tf_op jit(solution)/shard_map/dsgd/pallas_call | solution.py:338
  121.5 0.6 copy.9
  122.1 0.6 copy.10

commit v8 on v7

--- a/solution.py
+++ b/solution.py
@@ -97,8 +97,10 @@
     far_0 = lax.rem(lead + 1, nb)
     far_1 = lax.rem(lead + 2, nb)
     late = nb - 2
-    direct = [w for w in range(nb) if w != late]
-    parts = hop_1.shape[1]
+    last = nb - 1
+    depth = hop_1.shape[2]
+    pieces = [(late, c) for c in range(r_all.shape[2] // depth)] + [(last, 0)]
+    rest = pl.ds(depth, r_all.shape[2] - depth)
     rows, cols = r_all.shape[2:]
     subs = lr.shape[1]
     half = cols // 2
@@ -154,28 +156,32 @@
         get_results()
 
     def part_rows(c):
-        return pl.ds(c * hop_1.shape[2], hop_1.shape[2])
+        return pl.ds(c * depth, depth)
 
     def send_far(side):
         cps = send_factors()
         cps.append(send_block(0))
-        for c in range(parts):
+        for n, (w, c) in enumerate(pieces):
+            if c == 0:
+                encode(w)
             cps.append(pltpu.make_async_remote_copy(
-                r_own.at[late, part_rows(c)], hop_1.at[side, c], h1s_sem.at[c], h1_sem.at[side, c],
+                r_own.at[w, part_rows(c)], hop_1.at[side, n], h1s_sem.at[n], h1_sem.at[side, n],
                 **device(other, 2 * other),
             ))
             cps[-1].start()
-        for w in direct[1:]:
+        for w in range(1, late):
             encode(w)
-        for w in direct[1:]:
             cps.append(send_block(w))
+        cps.append(pltpu.make_async_remote_copy(
+            r_own.at[last, rest], r_all.at[last, me, rest], s_sem.at[last], r_sem.at[last, me], **device(rep, lead)
+        ))
+        cps[-1].start()
         return cps
 
     @pl.when(me == far_0)
     def _():
         tell((rep, lead))
         encode(0)
-        encode(late)
         pl.semaphore_wait(barrier, 2)
         finish(send_far(0))
 
@@ -183,7 +189,6 @@
     def _():
         tell((rep, lead))
         encode(0)
-        encode(late)
         pl.semaphore_wait(barrier, 2)
         finish(send_far(1))
 
@@ -199,12 +204,12 @@
             encode(w)
         for w in range(1, nb):
             cps.append(send_block(w))
-        for c in range(parts):
+        for n, (w, c) in enumerate(pieces):
             for side in range(2):
-                pltpu.make_async_copy(hop_1.at[side, c], hop_1.at[side, c], h1_sem.at[side, c]).wait()
+                pltpu.make_async_copy(hop_1.at[side, n], hop_1.at[side, n], h1_sem.at[side, n]).wait()
                 home = lax.rem(2 * other + 2 + side, nb)
                 cps.append(pltpu.make_async_remote_copy(
-                    hop_1.at[side, c], r_all.at[late, home, part_rows(c)], h2s_sem.at[side, c], h3_sem.at[side, c],
+                    hop_1.at[side, n], r_all.at[w, home, part_rows(c)], h2s_sem.at[side, n], h3_sem.at[side, n],
                     **device(other, 2 * other + 1),
                 ))
                 cps[-1].start()
@@ -276,17 +281,22 @@
         def first_epoch(w, carry):
             pltpu.make_async_copy(r_all.at[w, mate], r_all.at[w, mate], r_sem.at[w, mate]).wait()
 
-            @pl.when(w != late)
+            @pl.when(w < late)
             def _():
                 for j in (far_0, far_1):
                     pltpu.make_async_copy(r_all.at[w, j], r_all.at[w, j], r_sem.at[w, j]).wait()
 
-            @pl.when(w == late)
-            def _():
-                for c in range(parts):
+            for row in (late, last):
+                @pl.when(w == row)
+                def _():
                     for side, j in enumerate((far_0, far_1)):
-                        dst = r_all.at[late, j, part_rows(c)]
-                        pltpu.make_async_copy(dst, dst, h3_sem.at[side, c]).wait()
+                        for n, (at, c) in enumerate(pieces):
+                            if at == row:
+                                dst = r_all.at[row, j, part_rows(c)]
+                                pltpu.make_async_copy(dst, dst, h3_sem.at[side, n]).wait()
+                        if row == last:
+                            dst = r_all.at[last, j, rest]
+                            pltpu.make_async_copy(dst, dst, r_sem.at[last, j]).wait()
 
             for j in (mate, far_0, far_1):
                 coded = r_all[w, j]
@@ -345,7 +355,7 @@
                 pltpu.VMEM((nb, nb, rows, cols), BF16),
                 pltpu.VMEM((nb, rows, cols), F32),
                 pltpu.VMEM((nb, rows, cols), jnp.int32),
-                pltpu.VMEM((2, 4, rows // 4, cols), F32),
+                pltpu.VMEM((2, 5, rows // 4, cols), F32),
                 pltpu.VMEM((nb, rank, rows), F32),
                 pltpu.VMEM((nb, rank, cols), F32),
                 pltpu.VMEM((nb, rows, KPAD), F32),
@@ -357,7 +367,7 @@
                 dma((nb, nb)), dma((nb,)), dma((nb,)), dma((nb,)), dma, dma,
                 dma, dma, dma((nb - 1,)), dma((nb - 1,)),
                 pltpu.SMEM((STEPS, subs), F32), dma,
-                dma((2, 4)), dma((4,)), dma((2, 4)), dma((2, 4)),
+                dma((2, 5)), dma((5,)), dma((2, 5)), dma((2, 5)),
             ],
             compiler_params=pltpu.CompilerParams(collective_id=0, has_side_effects=True),
             name="dsgd",

time: 123 us -> 122 us (level)
  no operation moved by 1% of the time
where the time goes in v8:
time: 122 us
  Pallas kernels  120 us (98%)
  local copies, waits for them, and re-layouts  1.26 us (1%)
    pallas_call x1, Pallas kernels, local_run(): pl.pallas_call(functools.partial(kernel, nb, rank, base_eta), out_shape=(...  120 us

profile of v8, /device:TPU:1, one launch (start us, length us, event | category | flops | bytes accessed | tf_op | source)
XLA Modules:
  0.0 121.9 jit_solution(2922784968055753180)
XLA Ops:
  0.6 120.0 %dsgd.1 = (f32[50,128]{1,0:T(8,128)S(1)}, f32[50,512]{1,0:T(8,128)S(1)}) custom-call(f32[4,64]{1,0:T(4,128)} %bitcast.9, f32[512,512]{1,0:T(8,128)} %rate.1, s32[512,512]{1,0:T(8,128)} %mask.1, f32[50,128]{1,0:T(8,128)} %bitcast.8, f32[50,512]{1,0:T(8,128)} %bitcast.7), custom_call_target="tpu_custom_call" | custom-call | tf_op jit(solution)/shard_map/dsgd/pallas_call | solution.py:348
  120.6 0.6 copy.9
  121.2 0.6 copy.10

commit v9 on v8

--- a/solution.py
+++ b/solution.py
@@ -12,7 +12,7 @@
 LAMBDA = 0.05
 STEPS = 4
 KPAD = 64
-UNROLL = 12
+UNROLL = 20
 LEN_A, LEN_B, A_TO_B, B_TO_C, LEN_C = 64, 96, 226, 211, 35
 F32 = jnp.float32
 BF16 = jnp.bfloat16

time: 122 us -> 122 us (level)
  no operation moved by 1% of the time
where the time goes in v9:
time: 122 us
  Pallas kernels  120 us (98%)
  local copies, waits for them, and re-layouts  1.26 us (1%)
    pallas_call x1, Pallas kernels, local_run(): pl.pallas_call(functools.partial(kernel, nb, rank, base_eta), out_shape=(...  120 us

profile of v9, /device:TPU:1, one launch (start us, length us, event | category | flops | bytes accessed | tf_op | source)
XLA Modules:
  0.0 121.7 jit_solution(2866901438812127023)
XLA Ops:
  0.6 119.8 %dsgd.1 = (f32[50,128]{1,0:T(8,128)S(1)}, f32[50,512]{1,0:T(8,128)S(1)}) custom-call(f32[4,64]{1,0:T(4,128)} %bitcast.9, f32[512,512]{1,0:T(8,128)} %rate.1, s32[512,512]{1,0:T(8,128)} %mask.1, f32[50,128]{1,0:T(8,128)} %bitcast.8, f32[50,512]{1,0:T(8,128)} %bitcast.7), custom_call_target="tpu_custom_call" | custom-call | tf_op jit(solution)/shard_map/dsgd/pallas_call | solution.py:348
  120.4 0.6 copy.9
  121.1 0.6 copy.10
